TPU v7x, 32 devices: a whole 2x2x4 slice. The times are simulated.
32 devices in a mesh: len: 2 (over x), wid: 4 (over z), dep: 4 (over y, core).
Axes of the slice: x: 2, y: 2, z: 4, core: 2. Of those that a mesh axis runs over, the one named last changes fastest.
Arguments:
- coords: float32 [3, 32768], P(None, ('len', 'wid', 'dep')), may hold values from -3 to 3
- velocity: float32 [3, 32768], P(None, ('len', 'wid', 'dep')), may hold values from -6 to 6
- node_mass: float32 [32768], P(('len', 'wid', 'dep')), may hold values from 0.5 to 2
- corner_nodes: int32 [4, 32768], P(None, ('len', 'wid', 'dep')), may hold values from 0 to 1151, as said below
- shape_grad: float32 [8, 32768], P(None, ('len', 'wid', 'dep')), may hold values from -5 to 5
- frame_angles: float32 [2, 32768], P(None, ('len', 'wid', 'dep')), may hold values from -3.140625 to 3.140625
- volume: float32 [32768], P(('len', 'wid', 'dep')), may hold values from 0.5 to 2
- stress: float32 [3, 32768], P(None, ('len', 'wid', 'dep')), may hold values from -5 to 5
- send_nodes: int32 [32, 16, 256], P(('len', 'wid', 'dep')), may hold values from 0 to 1023
- tile_count: int32 [32], P(('len', 'wid', 'dep')), may hold values from 1 to 4, as said below
- tile_nodes: int32 [128, 128], P(('len', 'wid', 'dep')), may hold values from 0 to 4095
- tile_facets: int32 [4, 128, 128], P(None, ('len', 'wid', 'dep')), may hold values from 0 to 4095
- pair_mask: int32 [128, 128, 128], P(('len', 'wid', 'dep')), may hold values 0 or 1
Outputs:
- coords_out: float32 [3, 32768], P(None, ('len', 'wid', 'dep'))
- velocity_out: float32 [3, 32768], P(None, ('len', 'wid', 'dep'))
- stress_out: float32 [3, 32768], P(None, ('len', 'wid', 'dep'))
Inputs may be any that keep to these rules, and one draw needn't show every extreme that they name: `corner_nodes`: for the element at device-local position i (i = e mod 1024), every entry lies from (i // 128) * 128 to (i // 128) * 128 + 2 * 128 - 1. An entry j below 1024 names the element device's own node j; an entry 1024 + i names node i of the next device in the order len, wid, dep, the last device's next being the first. `send_nodes`: entry [p, g, k] is a node of device p, by its local number, sent to device g of p's slab; nodes may repeat. `tile_count`: some device has 4 live tiles in every draw; a device's tiles at and past its count are not used. `tile_nodes`: slot g * 256 + k of the tile's device is slot k of what device g of its slab sends it. `tile_facets`: slots as for tile_nodes, one for each of a facet's four corners.
All inputs are finite; a program needn't handle non-finite values. No bound on the sum of `pair_mask` on one device may be relied on, other than what follows from the above.
Results may differ from a plain program's by a relative error of at most 0.0003.
Values sent between devices are 32-bit elements; how exact they have to be, the bound alone decides.
A program may use at most 64 MiB of HBM per device.

v0:
```python
import math
import jax
import jax.numpy as jnp
from jax import lax
from jax.sharding import PartitionSpec as P

RIM = 128
STEPS = 2
TIME_STEP = 0.1
YOUNG_MOD = 1.0
POISSON = 0.3
HOURGLASS = 0.1
RADIUS_SQ = 1.0
STIFFNESS = 0.1
DAMPING = 0.05


def from_behind(value, axis, steps):
    count = lax.axis_size(axis)
    pairs = [(source, (source + steps) % count) for source in range(count)]
    return lax.ppermute(value, axis, pairs)


def frame_vectors(frame_angles):
    polar_angle = frame_angles[0]
    azimuth = frame_angles[1]
    axis_one = jnp.stack(
        [
            jnp.cos(polar_angle) * jnp.cos(azimuth),
            jnp.cos(polar_angle) * jnp.sin(azimuth),
            -jnp.sin(polar_angle),
        ]
    )
    axis_two = jnp.stack([-jnp.sin(azimuth), jnp.cos(azimuth), jnp.zeros_like(azimuth)])
    return (axis_one, axis_two)


def element_forces(corner_vel, shape_grad, axis_one, axis_two, volume, stress):
    grad_x = shape_grad[:4]
    grad_y = shape_grad[4:]
    along_one = jnp.sum(axis_one[:, None, :] * corner_vel, axis=0)
    along_two = jnp.sum(axis_two[:, None, :] * corner_vel, axis=0)
    rate_xx = jnp.sum(grad_x * along_one, axis=0)
    rate_yy = jnp.sum(grad_y * along_two, axis=0)
    rate_xy = jnp.sum(grad_y * along_one + grad_x * along_two, axis=0)
    factor = TIME_STEP * YOUNG_MOD / (1.0 - POISSON * POISSON)
    sigma_xx = stress[0] + factor * (rate_xx + POISSON * rate_yy)
    sigma_yy = stress[1] + factor * (POISSON * rate_xx + rate_yy)
    sigma_xy = stress[2] + factor * 0.5 * (1.0 - POISSON) * rate_xy
    hourglass_mode = jnp.array([1.0, -1.0, 1.0, -1.0], jnp.float32)[:, None]
    hourglass_rate = jnp.sum(hourglass_mode[None] * corner_vel, axis=1)
    force_one = -volume * (grad_x * sigma_xx + grad_y * sigma_xy)
    force_two = -volume * (grad_y * sigma_yy + grad_x * sigma_xy)
    corner_force = (
        axis_one[:, None] * force_one[None]
        + axis_two[:, None] * force_two[None]
        - HOURGLASS * volume * hourglass_mode[None] * hourglass_rate[:, None]
    )
    return (corner_force, jnp.stack([sigma_xx, sigma_yy, sigma_xy]))


def tile_forces(node_coordinates, node_velocities, corner_pos, corner_vel, pair_bits, live_row):
    facet_centroid = 0.25 * jnp.sum(corner_pos, axis=1)
    centroid_velocity = 0.25 * jnp.sum(corner_vel, axis=1)
    inner_product = jnp.einsum(
        "ywq,ywk->wqk", node_coordinates, facet_centroid, precision=lax.Precision.HIGHEST
    )
    distance = (
        jnp.sum(node_coordinates * node_coordinates, axis=0)[:, :, None]
        + jnp.sum(facet_centroid * facet_centroid, axis=0)[:, None, :]
        - 2.0 * inner_product
    )
    corner_weight = (
        pair_bits.astype(jnp.float32)
        * live_row[:, None, None]
        * jnp.maximum(RADIUS_SQ - distance, 0.0)
    )
    row_sum = jnp.sum(corner_weight, axis=2)
    col_sum = jnp.sum(corner_weight, axis=1)
    gathered_positions = jnp.einsum(
        "yml,mjl->ymj", facet_centroid, corner_weight, precision=lax.Precision.HIGHEST
    )
    gathered_velocities = jnp.einsum(
        "yml,mjl->ymj", centroid_velocity, corner_weight, precision=lax.Precision.HIGHEST
    )
    node_force = STIFFNESS * (row_sum * node_coordinates - gathered_positions) - DAMPING * (
        row_sum * node_velocities - gathered_velocities
    )
    outgoing_positions = jnp.einsum(
        "ewo,woj->ewj", node_coordinates, corner_weight, precision=lax.Precision.HIGHEST
    )
    outgoing_velocities = jnp.einsum(
        "ewo,woj->ewj", node_velocities, corner_weight, precision=lax.Precision.HIGHEST
    )
    facet_force = STIFFNESS * (outgoing_positions - col_sum * facet_centroid) - DAMPING * (
        outgoing_velocities - col_sum * centroid_velocity
    )
    return (node_force, -0.25 * facet_force)


def split_parts(values):
    first = lax.optimization_barrier(values.astype(jnp.bfloat16))
    rest = values - first.astype(jnp.float32)
    second = lax.optimization_barrier(rest.astype(jnp.bfloat16))
    third = (rest - second.astype(jnp.float32)).astype(jnp.bfloat16)
    return jnp.concatenate([first, second, third], axis=0)


def put_rows(values, index, total):
    chans, count = values.shape
    low_span = math.gcd(total, 128)
    high_span = total // low_span
    block = math.gcd(count, 1024)
    turns = count // block
    parts = jnp.transpose(split_parts(values).reshape(3 * chans, turns, block), (1, 0, 2))
    index_blocks = index.reshape(turns, block)
    low_iota = jnp.arange(low_span, dtype=jnp.int32)
    high_iota = jnp.arange(high_span, dtype=jnp.int32)

    def add_block(running, pieces):
        part, ids = pieces
        low_match = ids[:, None] % low_span == low_iota[None, :]
        spread_rows = jnp.where(low_match[None], part[:, :, None], jnp.zeros((), jnp.bfloat16))
        high_match = (ids[:, None] // low_span == high_iota[None, :]).astype(jnp.bfloat16)
        return (
            running
            + jnp.einsum(
                "mh,kml->khl", high_match, spread_rows, preferred_element_type=jnp.float32
            ),
            None,
        )

    summed, unused = lax.scan(
        add_block, jnp.zeros((3 * chans, high_span, low_span), jnp.float32), (parts, index_blocks)
    )
    return summed.reshape(3, chans, total).sum(axis=0)


def window_layout(corner_nodes, span):
    elements = corner_nodes.shape[1]
    blocks = elements // span
    group = math.gcd(blocks, 8)
    rounds = blocks // group
    starts = (jnp.arange(blocks, dtype=jnp.int32) * span)[None, :, None]
    local_ids = (corner_nodes.reshape(4, blocks, span) - starts).reshape(4, rounds, group, span)
    return (jnp.transpose(local_ids, (1, 0, 2, 3)), blocks, group, rounds)


def window_gather(extended, corner_nodes, span):
    local_ids, blocks, group, rounds = window_layout(corner_nodes, span)
    pieces = extended.reshape(3, blocks + 1, span)
    windows = jnp.concatenate([pieces[:, :-1], pieces[:, 1:]], axis=2)
    parts = jnp.transpose(split_parts(windows).reshape(9, rounds, group, 2 * span), (1, 0, 2, 3))
    window_iota = jnp.arange(2 * span, dtype=jnp.int32)

    def pick_round(items):
        part, ids = items
        onehot = (ids[..., None] == window_iota).astype(jnp.bfloat16)
        return jnp.einsum("abij,kbj->kabi", onehot, part, preferred_element_type=jnp.float32)

    picked = lax.map(pick_round, (parts, local_ids))
    picked = jnp.transpose(picked, (1, 2, 0, 3, 4)).reshape(3, 3, 4, blocks * span)
    return picked.sum(axis=0)


def window_put(corner_force, corner_nodes, span):
    local_ids, blocks, group, rounds = window_layout(corner_nodes, span)
    parts = jnp.transpose(
        split_parts(corner_force).reshape(9, 4, rounds, group, span), (2, 0, 1, 3, 4)
    )
    window_iota = jnp.arange(2 * span, dtype=jnp.int32)

    def put_round(items):
        part, ids = items
        onehot = (ids[..., None] == window_iota).astype(jnp.bfloat16)
        return jnp.einsum("abij,kabi->kbj", onehot, part, preferred_element_type=jnp.float32)

    sums = lax.map(put_round, (parts, local_ids))
    sums = jnp.transpose(sums, (1, 0, 2, 3)).reshape(3, 3, blocks, 2 * span).sum(axis=0)
    near_half = jnp.pad(sums[:, :, :span], ((0, 0), (0, 1), (0, 0)))
    far_half = jnp.pad(sums[:, :, span:], ((0, 0), (1, 0), (0, 0)))
    return (near_half + far_half).reshape(3, (blocks + 1) * span)


def spread_tiles(node_force, facet_share, tile_nodes, tile_facets, total):
    corner_share = jnp.broadcast_to(facet_share[:, None], (3, 4) + facet_share.shape[1:])
    values = jnp.concatenate([node_force.reshape(3, -1), corner_share.reshape(3, -1)], axis=1)
    index = jnp.concatenate([tile_nodes.reshape(-1), tile_facets.reshape(-1)], axis=0)
    return put_rows(values, index, total)


def ship_out(positions, velocities):
    recv_pos, recv_vel = (
        lax.all_to_all(positions, ("wid", "dep"), split_axis=1, concat_axis=1, tiled=True),
        lax.all_to_all(velocities, ("wid", "dep"), split_axis=1, concat_axis=1, tiled=True),
    )
    return (recv_pos.reshape(3, -1), recv_vel.reshape(3, -1))


def ship_back(buffer, capacity):
    group_size = lax.axis_size("wid") * lax.axis_size("dep")
    returned = lax.all_to_all(
        buffer.reshape(3, group_size, capacity),
        ("wid", "dep"),
        split_axis=1,
        concat_axis=1,
        tiled=True,
    )
    return returned


def contact_buffer(recv_pos, recv_vel, tile_nodes, tile_facets, pair_mask, live_tiles):
    total = recv_pos.shape[1]
    node_force, facet_share = tile_forces(
        recv_pos[:, tile_nodes],
        recv_vel[:, tile_nodes],
        recv_pos[:, tile_facets],
        recv_vel[:, tile_facets],
        pair_mask,
        live_tiles,
    )
    return spread_tiles(node_force, facet_share, tile_nodes, tile_facets, total)


def per_device(
    coords,
    velocity,
    node_mass,
    corner_nodes,
    shape_grad,
    frame_angles,
    volume,
    stress,
    send_nodes,
    tile_count,
    tile_nodes,
    tile_facets,
    pair_mask,
):
    axis_one, axis_two = frame_vectors(frame_angles)
    slot_rows = send_nodes[0]
    capacity = slot_rows.shape[1]
    slot_flat = slot_rows.reshape(-1)
    tile_slots = pair_mask.shape[0]
    live_tiles = (jnp.arange(tile_slots, dtype=jnp.int32) < tile_count[0]).astype(jnp.float32)
    local_count = coords.shape[1]
    for repeat in range(STEPS):
        ghosts = from_behind(velocity[:, :RIM], ("len", "wid", "dep"), -1)
        extended = jnp.concatenate([velocity, ghosts], axis=1)
        corner_vel = window_gather(extended, corner_nodes, RIM)
        corner_force, stress = element_forces(
            corner_vel, shape_grad, axis_one, axis_two, volume, stress
        )
        nodal_sum = window_put(corner_force, corner_nodes, RIM)
        returned = from_behind(nodal_sum[:, local_count:], ("len", "wid", "dep"), 1)
        internal = nodal_sum[:, :local_count] + jnp.pad(returned, ((0, 0), (0, local_count - RIM)))
        recv_pos, recv_vel = ship_out(coords[:, slot_rows], velocity[:, slot_rows])
        buffer = contact_buffer(recv_pos, recv_vel, tile_nodes, tile_facets, pair_mask, live_tiles)
        answer = ship_back(buffer, capacity)
        contact = put_rows(answer.reshape(3, -1), slot_flat, local_count)
        velocity = velocity + TIME_STEP * (internal + contact) / node_mass
        coords = coords + TIME_STEP * velocity
    return (coords, velocity, stress)


def solution(mesh):
    placed = (
        P(None, ("len", "wid", "dep")),
        P(None, ("len", "wid", "dep")),
        P(("len", "wid", "dep")),
        P(None, ("len", "wid", "dep")),
        P(None, ("len", "wid", "dep")),
        P(None, ("len", "wid", "dep")),
        P(("len", "wid", "dep")),
        P(None, ("len", "wid", "dep")),
        P(("len", "wid", "dep"), None, None),
        P(("len", "wid", "dep")),
        P(("len", "wid", "dep"), None),
        P(None, ("len", "wid", "dep"), None),
        P(("len", "wid", "dep"), None, None),
    )
    return jax.shard_map(
        per_device,
        mesh=mesh,
        in_specs=placed,
        out_specs=(
            P(None, ("len", "wid", "dep")),
            P(None, ("len", "wid", "dep")),
            P(None, ("len", "wid", "dep")),
        ),
        check_vma=False,
    )
```

profile of v0, /device:TPU:0, one launch (start us, length us, event | category | flops | bytes accessed | tf_op | source)
XLA Modules:
  0.0 197.0 jit_solution(1197763720123110898)
XLA Ops:
  0.7 1.0 copy.159
  2.4 10.8 %gather_fusion = f32[4096,3]{1,0:T(8,128)S(1)} fusion(f32[3,1024]{0,1:T(8,128)S(1)} %copy.159, s32[4096]{0:T(1024)S(1)} %broadcast_clamp_fusion), kind=kCustom, calls=%fused_computation | custom fusion | bytes 114688 | tf_op jit(solution)/shard_map/gather | solution.py:257
  13.2 1.2 copy.160
  14.5 7.4 %all-to-all-start = ((f32[3,16,256]{2,0,1:T(4,128)}), f32[3,16,256]{2,0,1:T(4,128)S(1)}, u32[]{:S(2)}, u32[]{:S(2)}) async-start(f32[3,16,256]{2,0,1:T(4,128)} %bitcast.19), calls=%async_computation | async-start | bytes 131072 | tf_op jit(solution)/shard_map/all_to_all | solution.py:194
  21.9 5.3 %collective-permute-start = (f32[3,128]{1,0:T(4,128)S(1)}, f32[3,128]{1,0:T(4,128)S(1)}, u32[]{:S(2)}, u32[]{:S(2)}) collective-permute-start(f32[3,128]{1,0:T(4,128)S(1)} %slice.69), channel_id=1, source_target_pairs={{0,31},{1,0},{2,1},{3,2},{4,3},{5,4},{6,5},{7,6},{8,7},{9,8},{10,9... | collective-permute-start | bytes 4616 | tf_op jit(solution)/shard_map/ppermute | solution.py:21
  30.5 10.8 %gather_fusion.3 = f32[4096,3]{1,0:T(8,128)S(1)} fusion(f32[3,1024]{0,1:T(8,128)S(1)} %copy.166, s32[4096]{0:T(1024)S(1)} %broadcast_clamp_fusion), kind=kCustom, calls=%fused_computation.3 | custom fusion | bytes 114688 | tf_op jit(solution)/shard_map/gather | solution.py:257
  41.3 1.2 copy.167
  42.7 1.4 fusion.100
  45.3 1.4 fusion.102
  47.4 3.5 %all-to-all-start.1 = ((f32[3,16,256]{2,0,1:T(4,128)}), f32[3,16,256]{2,0,1:T(4,128)S(1)}, u32[]{:S(2)}, u32[]{:S(2)}) async-start(f32[3,16,256]{2,0,1:T(4,128)} %bitcast.29), calls=%async_computation.1 | async-start | bytes 131072 | tf_op jit(solution)/shard_map/all_to_all | solution.py:195
  51.6 5.5 %gather_fusion.2 = f32[2048,3]{1,0:T(8,128)S(1)} fusion(f32[3,4096]{0,1:T(8,128)S(1)} %bitcast.286, s32[2048]{0:T(1024)S(1)} %broadcast_clamp_fusion.1), kind=kCustom, calls=%fused_computation.2 | custom fusion | bytes 57344 | tf_op jit(solution)/shard_map/gather | solution.py:217
  57.1 1.8 gather_fusion.1
  61.1 1.6 gather_fusion.4
  62.7 5.5 %gather_fusion.5 = f32[2048,3]{1,0:T(8,128)S(1)} fusion(f32[3,4096]{0,1:T(8,128)S(1)} %bitcast.291, s32[2048]{0:T(1024)S(1)} %broadcast_clamp_fusion.1), kind=kCustom, calls=%fused_computation.5 | custom fusion | bytes 57344 | tf_op jit(solution)/shard_map/gather | solution.py:218
  68.2 1.1 copy.163
  69.3 1.8 fusion.202
  71.0 1.1 copy.170
  74.5 8.7 %while.68 = (s32[]{:T(128)}, f32[9,32,128]{2,1,0:T(8,128)S(1)}, s32[5,512]{1,0:T(8,128)}, bf16[5,9,512]{2,1,0:T(8,128)(2,1)S(1)}, s32[]{:T(128)}, /*index=5*/s32[]{:T(128)}) while((s32[]{:T(128)}, f32[9,32,128]{2,1,0:T(8,128)S(1)}, s32[5,512]{1,0:T(8,128)}, bf16[5,9,512]{2,1,0:T(8,128)(2,1)S(1)}, s32[]{:T(128)}, ...), condition=%wide.region_15.16_spmd.clone, body=%wide.region_14.15_spmd.clone.sunk | while | flops 38503936 | bytes 468063 | solution.py:133
  74.5 0.7 constant_dynamic-slice_fusion.8
  75.4 0.8 fusion.232
  76.2 0.7 constant_dynamic-slice_fusion.8
  77.2 0.8 fusion.232
  78.0 0.7 constant_dynamic-slice_fusion.8
  78.9 0.8 fusion.232
  80.6 0.8 fusion.232
  82.4 0.8 fusion.232
  84.0 6.0 %all-to-all-start.2 = ((f32[3,16,256]{2,0,1:T(4,128)}), f32[3,16,256]{2,0,1:T(4,128)S(1)}, u32[]{:S(2)}, u32[]{:S(2)}) async-start(f32[3,16,256]{2,0,1:T(4,128)} %bitcast.39), calls=%async_computation.2 | async-start | bytes 131072 | tf_op jit(solution)/shard_map/all_to_all | solution.py:202
  90.5 6.4 %all-to-all-done.2 = f32[3,16,256]{2,0,1:T(4,128)S(1)} async-done(((f32[3,16,256]{2,0,1:T(4,128)}), f32[3,16,256]{2,0,1:T(4,128)S(1)}, u32[]{:S(2)}, u32[]{:S(2)}) %all-to-all-start.2) | async-done | bytes 49184 | tf_op jit(solution)/shard_map/all_to_all | solution.py:202
  97.1 6.7 %while.69 = (s32[]{:T(128)}, f32[9,8,128]{2,1,0:T(8,128)S(1)}, s32[4,1024]{1,0:T(4,128)S(1)}, bf16[4,9,1024]{2,1,0:T(8,128)(2,1)S(1)}, s32[]{:T(128)}, /*index=5*/s32[]{:T(128)}) while((s32[]{:T(128)}, f32[9,8,128]{2,1,0:T(8,128)S(1)}, s32[4,1024]{1,0:T(4,128)S(1)}, bf16[4,9,1024]{2,1,0:T(8,128)(2,1)S(1)}, s32[]{:T(128)}, ...), condition=%wide.region_18.19_spmd.clone, body=%wide.region_17.18_spmd.clone.sunk | while | flops 20231172 | bytes 419935 | solution.py:133
  97.4 1.4 fusion.235
  99.1 1.4 fusion.235
  100.7 1.4 fusion.235
  102.4 1.4 fusion.235
  104.8 10.8 %gather_fusion.6 = f32[4096,3]{1,0:T(8,128)S(1)} fusion(f32[3,1024]{0,1:T(8,128)S(1)} %copy.182, s32[4096]{0:T(1024)S(1)} %broadcast_clamp_fusion), kind=kCustom, calls=%fused_computation.6 | custom fusion | bytes 114688 | tf_op jit(solution)/shard_map/gather | solution.py:257
  115.6 1.2 copy.183
  116.8 3.7 %all-to-all-start.3 = ((f32[3,16,256]{2,0,1:T(4,128)}), f32[3,16,256]{2,0,1:T(4,128)S(1)}, u32[]{:S(2)}, u32[]{:S(2)}) async-start(f32[3,16,256]{2,0,1:T(4,128)} %bitcast.58), calls=%async_computation.3 | async-start | bytes 131072 | tf_op jit(solution)/shard_map/all_to_all | solution.py:194
  120.5 10.8 %gather_fusion.9 = f32[4096,3]{1,0:T(8,128)S(1)} fusion(f32[3,1024]{0,1:T(8,128)S(1)} %copy.189, s32[4096]{0:T(1024)S(1)} %broadcast_clamp_fusion), kind=kCustom, calls=%fused_computation.9 | custom fusion | bytes 114688 | tf_op jit(solution)/shard_map/gather | solution.py:257
  131.4 1.2 copy.190
  132.7 1.4 fusion.101
  135.1 1.4 fusion.103
  137.4 6.7 %all-to-all-start.4 = ((f32[3,16,256]{2,0,1:T(4,128)}), f32[3,16,256]{2,0,1:T(4,128)S(1)}, u32[]{:S(2)}, u32[]{:S(2)}) async-start(f32[3,16,256]{2,0,1:T(4,128)} %bitcast.66), calls=%async_computation.4 | async-start | bytes 131072 | tf_op jit(solution)/shard_map/all_to_all | solution.py:195
  144.7 5.5 %gather_fusion.8 = f32[2048,3]{1,0:T(8,128)S(1)} fusion(f32[3,4096]{0,1:T(8,128)S(1)} %bitcast.292, s32[2048]{0:T(1024)S(1)} %broadcast_clamp_fusion.1), kind=kCustom, calls=%fused_computation.8 | custom fusion | bytes 57344 | tf_op jit(solution)/shard_map/gather | solution.py:217
  150.2 1.6 gather_fusion.7
  152.9 1.6 gather_fusion.10
  154.5 5.5 %gather_fusion.11 = f32[2048,3]{1,0:T(8,128)S(1)} fusion(f32[3,4096]{0,1:T(8,128)S(1)} %bitcast.289, s32[2048]{0:T(1024)S(1)} %broadcast_clamp_fusion.1), kind=kCustom, calls=%fused_computation.11 | custom fusion | bytes 57344 | tf_op jit(solution)/shard_map/gather | solution.py:218
  160.0 1.1 copy.186
  161.1 1.8 fusion.201
  162.8 1.1 copy.193
  166.2 8.7 %while.70 = (s32[]{:T(128)}, f32[9,32,128]{2,1,0:T(8,128)S(1)}, s32[5,512]{1,0:T(8,128)}, bf16[5,9,512]{2,1,0:T(8,128)(2,1)S(1)}, s32[]{:T(128)}, /*index=5*/s32[]{:T(128)}) while((s32[]{:T(128)}, f32[9,32,128]{2,1,0:T(8,128)S(1)}, s32[5,512]{1,0:T(8,128)}, bf16[5,9,512]{2,1,0:T(8,128)(2,1)S(1)}, s32[]{:T(128)}, ...), condition=%wide.region_35.36_spmd.clone, body=%wide.region_34.35_spmd.clone.sunk | while | flops 38503936 | bytes 468063 | solution.py:133
  167.2 0.8 fusion.238
  168.9 0.8 fusion.238
  169.7 0.7 constant_dynamic-slice_fusion.10
  170.7 0.8 fusion.238
  172.4 0.8 fusion.238
  173.2 0.7 constant_dynamic-slice_fusion.10
  174.1 0.8 fusion.238
  175.7 6.0 %all-to-all-start.5 = ((f32[3,16,256]{2,0,1:T(4,128)}), f32[3,16,256]{2,0,1:T(4,128)S(1)}, u32[]{:S(2)}, u32[]{:S(2)}) async-start(f32[3,16,256]{2,0,1:T(4,128)} %bitcast.76), calls=%async_computation.5 | async-start | bytes 131072 | tf_op jit(solution)/shard_map/all_to_all | solution.py:202
  182.4 6.3 %all-to-all-done.5 = f32[3,16,256]{2,0,1:T(4,128)S(1)} async-done(((f32[3,16,256]{2,0,1:T(4,128)}), f32[3,16,256]{2,0,1:T(4,128)S(1)}, u32[]{:S(2)}, u32[]{:S(2)}) %all-to-all-start.5) | async-done | bytes 49184 | tf_op jit(solution)/shard_map/all_to_all | solution.py:202
  188.9 6.7 %while.71 = (s32[]{:T(128)}, f32[9,8,128]{2,1,0:T(8,128)S(1)}, s32[4,1024]{1,0:T(4,128)S(1)}, bf16[4,9,1024]{2,1,0:T(8,128)(2,1)S(1)}, s32[]{:T(128)}, /*index=5*/s32[]{:T(128)}) while((s32[]{:T(128)}, f32[9,8,128]{2,1,0:T(8,128)S(1)}, s32[4,1024]{1,0:T(4,128)S(1)}, bf16[4,9,1024]{2,1,0:T(8,128)(2,1)S(1)}, s32[]{:T(128)}, ...), condition=%wide.region_38.39_spmd.clone, body=%wide.region_37.38_spmd.clone.sunk | while | flops 20231172 | bytes 419935 | solution.py:133
  189.2 1.4 fusion.241
  190.9 1.4 fusion.241
  192.5 1.4 fusion.241
  194.2 1.4 fusion.241
  195.7 1.3 multiply_add_fusion
  (307 shorter events, 27.0 us)
Async XLA Ops:
  0.6 29.0 %copy-start.14 = (s32[1,16,256]{2,1,0:T(8,128)S(1)}, s32[1,16,256]{2,1,0:T(8,128)}, u32[]{:S(2)}) copy-start(s32[1,16,256]{2,1,0:T(8,128)} %param.31) | copy-start | bytes 49156
  0.6 21.2 %copy-start.1 = (f32[3,1024]{1,0:T(4,128)S(1)}, f32[3,1024]{1,0:T(4,128)}, u32[]{:S(2)}) copy-start(f32[3,1024]{1,0:T(4,128)} %param.24) | copy-start | bytes 36868
  0.7 26.6 %copy-start.28 = (s32[4,4,128]{2,1,0:T(4,128)S(1)}, s32[4,4,128]{2,1,0:T(4,128)}, u32[]{:S(2)}) copy-start(s32[4,4,128]{2,1,0:T(4,128)} %param.34) | copy-start | bytes 24580
  0.7 26.6 %copy-start.38 = (s32[4,128]{1,0:T(4,128)S(1)}, s32[4,128]{1,0:T(4,128)}, u32[]{:S(2)}) copy-start(s32[4,128]{1,0:T(4,128)} %param.33) | copy-start | bytes 6148
  0.7 27.8 %copy-start.37 = (f32[2,1024]{1,0:T(2,128)S(1)}, f32[2,1024]{1,0:T(2,128)}, u32[]{:S(2)}) copy-start(f32[2,1024]{1,0:T(2,128)} %param.28) | copy-start | bytes 24580
  0.7 28.1 %copy-start.39 = (f32[1024]{0:T(1024)S(1)}, f32[1024]{0:T(1024)}, u32[]{:S(2)}) copy-start(f32[1024]{0:T(1024)} %param.29) | copy-start | bytes 12292
  0.7 28.1 %copy-start.33 = (s32[4,1024]{1,0:T(4,128)S(1)}, s32[4,1024]{1,0:T(4,128)}, u32[]{:S(2)}) copy-start(s32[4,1024]{1,0:T(4,128)} %param.26) | copy-start | bytes 49156
  14.5 33.0 %all-to-all-start = ((f32[3,16,256]{2,0,1:T(4,128)}), f32[3,16,256]{2,0,1:T(4,128)S(1)}, u32[]{:S(2)}, u32[]{:S(2)}) async-start(f32[3,16,256]{2,0,1:T(4,128)} %bitcast.19), calls=%async_computation | async-start | bytes 131072 | tf_op jit(solution)/shard_map/all_to_all | solution.py:194
  21.9 20.7 %collective-permute-start = (f32[3,128]{1,0:T(4,128)S(1)}, f32[3,128]{1,0:T(4,128)S(1)}, u32[]{:S(2)}, u32[]{:S(2)}) collective-permute-start(f32[3,128]{1,0:T(4,128)S(1)} %slice.69), channel_id=1, source_target_pairs={{0,31},{1,0},{2,1},{3,2},{4,3},{5,4},{6,5},{7,6},{8,7},{9,8},{10,9... | collective-permute-start | bytes 4616 | tf_op jit(solution)/shard_map/ppermute | solution.py:21
  29.0 16.1 %copy-start.3 = (f32[3,1024]{1,0:T(4,128)}, f32[3,1024]{1,0:T(4,128)S(1)}, u32[]{:S(2)}) copy-start(f32[3,1024]{1,0:T(4,128)S(1)} %pad_maximum_fusion.10) | copy-start | bytes 36868
  29.1 16.0 %copy-start.7 = (f32[3,1024]{1,0:T(4,128)}, f32[3,1024]{1,0:T(4,128)S(1)}, u32[]{:S(2)}) copy-start(f32[3,1024]{1,0:T(4,128)S(1)} %maximum_maximum_fusion) | copy-start | bytes 36868
  41.3 3.0 %copy-start = (f32[8,1024]{1,0:T(8,128)S(1)}, f32[8,1024]{1,0:T(8,128)}, u32[]{:S(2)}) copy-start(f32[8,1024]{1,0:T(8,128)} %param.27) | copy-start | bytes 98308
  41.3 3.1 %copy-start.36 = (f32[3,1024]{1,0:T(4,128)S(1)}, f32[3,1024]{1,0:T(4,128)}, u32[]{:S(2)}) copy-start(f32[3,1024]{1,0:T(4,128)} %param.30) | copy-start | bytes 36868
  41.3 3.1 %copy-start.41 = (f32[4]{0:T(128)S(1)}, f32[4]{0:T(128)}, u32[]{:S(2)}) copy-start(f32[4]{0:T(128)} %constant.306.clone) | copy-start | bytes 52
  42.6 4.2 %copy-start.34 = (s32[4,8,128]{2,0,1:T(4,128)}, s32[4,8,128]{2,0,1:T(4,128)S(1)}, u32[]{:S(2)}) copy-start(s32[4,8,128]{2,0,1:T(4,128)S(1)} %copy.155) | copy-start | bytes 49156
  44.4 0.6 copy-start.19
  44.5 0.6 copy-start.21
  44.6 0.6 copy-start.29
  47.4 13.0 %all-to-all-start.1 = ((f32[3,16,256]{2,0,1:T(4,128)}), f32[3,16,256]{2,0,1:T(4,128)S(1)}, u32[]{:S(2)}, u32[]{:S(2)}) async-start(f32[3,16,256]{2,0,1:T(4,128)} %bitcast.29), calls=%async_computation.1 | async-start | bytes 131072 | tf_op jit(solution)/shard_map/all_to_all | solution.py:195
  57.1 3.9 %copy-start.17 = (s32[1024]{0:T(1024)S(1)}, s32[1024]{0:T(1024)}, u32[]{:S(2)}) copy-start(s32[1024]{0:T(1024)} %pad_clamp_fusion) | copy-start | bytes 12292
  61.1 11.3 %copy-start.27 = (f32[4,128,3]{1,2,0:T(4,128)S(1)}, f32[4,128,3]{1,2,0:T(4,128)}, u32[]{:S(2)}) copy-start(f32[4,128,3]{1,2,0:T(4,128)} %copy.172) | copy-start | bytes 18436
  72.1 2.3 %copy-start.10 = (f32[9,32,128]{2,1,0:T(8,128)S(1)}, f32[9,32,128]{2,1,0:T(8,128)}, u32[]{:S(2)}) copy-start(f32[9,32,128]{2,1,0:T(8,128)} %custom-call) | copy-start | bytes 442372
  74.4 15.5 %copy-start.15 = (f32[3,8,128]{2,1,0:T(8,128)S(1)}, f32[3,8,128]{2,1,0:T(8,128)}, u32[]{:S(2)}) copy-start(f32[3,8,128]{2,1,0:T(8,128)} %get-tuple-element.600) | copy-start | bytes 36868
  74.5 15.5 %copy-start.16 = (f32[3,8,128]{2,1,0:T(8,128)S(1)}, f32[3,8,128]{2,1,0:T(8,128)}, u32[]{:S(2)}) copy-start(f32[3,8,128]{2,1,0:T(8,128)} %get-tuple-element.601) | copy-start | bytes 36868
  74.5 22.6 %copy-start.26 = (f32[9,8,128]{2,1,0:T(8,128)S(1)}, f32[9,8,128]{2,1,0:T(8,128)}, u32[]{:S(2)}) copy-start(f32[9,8,128]{2,1,0:T(8,128)} %custom-call.1) | copy-start | bytes 110596
  84.0 12.9 %all-to-all-start.2 = ((f32[3,16,256]{2,0,1:T(4,128)}), f32[3,16,256]{2,0,1:T(4,128)S(1)}, u32[]{:S(2)}, u32[]{:S(2)}) async-start(f32[3,16,256]{2,0,1:T(4,128)} %bitcast.39), calls=%async_computation.2 | async-start | bytes 131072 | tf_op jit(solution)/shard_map/all_to_all | solution.py:202
  90.0 13.9 %collective-permute-start.1 = (f32[3,128]{1,0:T(4,128)S(1)}, f32[3,128]{1,0:T(4,128)S(1)}, u32[]{:S(2)}, u32[]{:S(2)}) collective-permute-start(f32[3,128]{1,0:T(4,128)S(1)} %slice.115), channel_id=1, source_target_pairs={{0,1},{1,2},{2,3},{3,4},{4,5},{5,6},{6,7},{7,8},{8,9},{9,10},{10,1... | collective-permute-start | bytes 4616 | tf_op jit(solution)/shard_map/ppermute | solution.py:21
  97.1 6.8 %copy-start.2 = (f32[3,1024]{1,0:T(4,128)S(1)}, f32[3,1024]{1,0:T(4,128)}, u32[]{:S(2)}) copy-start(f32[3,1024]{1,0:T(4,128)} %param.24) | copy-start | bytes 36868
  97.1 6.8 %copy-start.13 = (f32[3,1024]{1,0:T(4,128)S(1)}, f32[3,1024]{1,0:T(4,128)}, u32[]{:S(2)}) copy-start(f32[3,1024]{1,0:T(4,128)} %param.23) | copy-start | bytes 36868
  97.1 6.8 %copy-start.31 = (f32[1024]{0:T(1024)S(1)}, f32[1024]{0:T(1024)}, u32[]{:S(2)}) copy-start(f32[1024]{0:T(1024)} %param.25) | copy-start | bytes 12292
  103.9 27.4 %copy-start.5 = (f32[3,1024]{1,0:T(4,128)}, f32[3,1024]{1,0:T(4,128)S(1)}, u32[]{:S(2)}) copy-start(f32[3,1024]{1,0:T(4,128)S(1)} %get-tuple-element.584) | copy-start | bytes 36868
  104.0 28.7 %collective-permute-start.2 = (f32[3,128]{1,0:T(4,128)S(1)}, f32[3,128]{1,0:T(4,128)S(1)}, u32[]{:S(2)}, u32[]{:S(2)}) collective-permute-start(f32[3,128]{1,0:T(4,128)S(1)} %slice.116), channel_id=1, source_target_pairs={{0,31},{1,0},{2,1},{3,2},{4,3},{5,4},{6,5},{7,6},{8,7},{9,8},{10,9... | collective-permute-start | bytes 4616 | tf_op jit(solution)/shard_map/ppermute | solution.py:21
  115.6 17.1 %copy-start.35 = (s32[4,8,128]{2,0,1:T(4,128)S(1)}, s32[4,8,128]{2,0,1:T(4,128)}, u32[]{:S(2)}) copy-start(s32[4,8,128]{2,0,1:T(4,128)} %copy-done.34) | copy-start | bytes 49156
  116.8 20.5 %all-to-all-start.3 = ((f32[3,16,256]{2,0,1:T(4,128)}), f32[3,16,256]{2,0,1:T(4,128)S(1)}, u32[]{:S(2)}, u32[]{:S(2)}) async-start(f32[3,16,256]{2,0,1:T(4,128)} %bitcast.58), calls=%async_computation.3 | async-start | bytes 131072 | tf_op jit(solution)/shard_map/all_to_all | solution.py:194
  131.3 3.0 %copy-start.4 = (f32[3,1024]{1,0:T(4,128)S(1)}, f32[3,1024]{1,0:T(4,128)}, u32[]{:S(2)}) copy-start(f32[3,1024]{1,0:T(4,128)} %copy-done.3) | copy-start | bytes 36868
  131.3 3.0 %copy-start.8 = (f32[3,1024]{1,0:T(4,128)S(1)}, f32[3,1024]{1,0:T(4,128)}, u32[]{:S(2)}) copy-start(f32[3,1024]{1,0:T(4,128)} %copy-done.7) | copy-start | bytes 36868
  131.3 3.1 %copy-start.20 = (f32[1,1024]{1,0:T(1,128)S(1)}, f32[1,1024]{1,0:T(1,128)}, u32[]{:S(2)}) copy-start(f32[1,1024]{1,0:T(1,128)} %copy-done.19) | copy-start | bytes 12292
  131.3 3.1 %copy-start.22 = (f32[1,1024]{1,0:T(1,128)S(1)}, f32[1,1024]{1,0:T(1,128)}, u32[]{:S(2)}) copy-start(f32[1,1024]{1,0:T(1,128)} %copy-done.21) | copy-start | bytes 12292
  131.4 3.2 %copy-start.30 = (f32[4,1024]{1,0:T(4,128)S(1)}, f32[4,1024]{1,0:T(4,128)}, u32[]{:S(2)}) copy-start(f32[4,1024]{1,0:T(4,128)} %copy-done.29) | copy-start | bytes 49156
  131.4 3.2 %copy-start.42 = (f32[4]{0:T(128)S(1)}, f32[4]{0:T(128)}, u32[]{:S(2)}) copy-start(f32[4]{0:T(128)} %constant.306.clone) | copy-start | bytes 52
  134.5 0.6 copy-start.23
  135.1 15.0 %copy-start.18 = (s32[1024]{0:T(1024)S(1)}, s32[1024]{0:T(1024)}, u32[]{:S(2)}) copy-start(s32[1024]{0:T(1024)} %pad_clamp_fusion) | copy-start | bytes 12292
  136.7 15.5 %copy-start.11 = (f32[1,3,9,128]{3,1,2,0:T(4,128)}, f32[1,3,9,128]{3,1,2,0:T(4,128)S(1)}, u32[]{:S(2)}) copy-start(f32[1,3,9,128]{3,1,2,0:T(4,128)S(1)} %copy.229) | copy-start | bytes 41476
  137.3 58.4 %collective-permute-start.3 = (f32[3,128]{1,0:T(4,128)}, f32[3,128]{1,0:T(4,128)}, u32[]{:S(2)}, u32[]{:S(2)}) collective-permute-start(f32[3,128]{1,0:T(4,128)} %slice.122), channel_id=1, source_target_pairs={{0,1},{1,2},{2,3},{3,4},{4,5},{5,6},{6,7},{7,8},{8,9},{9,10},{10,1... | collective-permute-start | bytes 4616 | tf_op jit(solution)/shard_map/ppermute | solution.py:21
  137.4 14.8 %all-to-all-start.4 = ((f32[3,16,256]{2,0,1:T(4,128)}), f32[3,16,256]{2,0,1:T(4,128)S(1)}, u32[]{:S(2)}, u32[]{:S(2)}) async-start(f32[3,16,256]{2,0,1:T(4,128)} %bitcast.66), calls=%async_computation.4 | async-start | bytes 131072 | tf_op jit(solution)/shard_map/all_to_all | solution.py:195
  151.8 9.2 %copy-start.40 = (f32[4]{0:T(128)S(1)}, f32[4]{0:T(128)}, u32[]{:S(2)}) copy-start(f32[4]{0:T(128)} %compare_convert_fusion) | copy-start | bytes 52
  163.9 2.3 %copy-start.9 = (f32[9,32,128]{2,1,0:T(8,128)S(1)}, f32[9,32,128]{2,1,0:T(8,128)}, u32[]{:S(2)}) copy-start(f32[9,32,128]{2,1,0:T(8,128)} %custom-call.2) | copy-start | bytes 442372
  166.2 15.5 %copy-start.24 = (f32[1,1024]{1,0:T(1,128)S(1)}, f32[1,1024]{1,0:T(1,128)}, u32[]{:S(2)}) copy-start(f32[1,1024]{1,0:T(1,128)} %copy-done.23) | copy-start | bytes 12292
  166.2 22.7 %copy-start.25 = (f32[9,8,128]{2,1,0:T(8,128)S(1)}, f32[9,8,128]{2,1,0:T(8,128)}, u32[]{:S(2)}) copy-start(f32[9,8,128]{2,1,0:T(8,128)} %custom-call.3) | copy-start | bytes 110596
  175.7 12.9 %all-to-all-start.5 = ((f32[3,16,256]{2,0,1:T(4,128)}), f32[3,16,256]{2,0,1:T(4,128)S(1)}, u32[]{:S(2)}, u32[]{:S(2)}) async-start(f32[3,16,256]{2,0,1:T(4,128)} %bitcast.76), calls=%async_computation.5 | async-start | bytes 131072 | tf_op jit(solution)/shard_map/all_to_all | solution.py:202
  188.9 6.8 %copy-start.6 = (f32[3,1024]{1,0:T(4,128)S(1)}, f32[3,1024]{1,0:T(4,128)}, u32[]{:S(2)}) copy-start(f32[3,1024]{1,0:T(4,128)} %copy-done.5) | copy-start | bytes 36868
  188.9 6.8 %copy-start.12 = (f32[1,3,9,128]{3,1,2,0:T(4,128)S(1)}, f32[1,3,9,128]{3,1,2,0:T(4,128)}, u32[]{:S(2)}) copy-start(f32[1,3,9,128]{3,1,2,0:T(4,128)} %copy-done.11) | copy-start | bytes 41476
  188.9 6.8 %copy-start.32 = (f32[1024]{0:T(1024)S(1)}, f32[1024]{0:T(1024)}, u32[]{:S(2)}) copy-start(f32[1024]{0:T(1024)} %param.25) | copy-start | bytes 12292
where the time goes:
time: 199 us; the launch traced here: 197 us
  local copies, waits for them, and re-layouts  97.6 us (49%)
  starting transfers between devices  39.5 us (20%)
  matrix products  32.1 us (16%)
  waiting for transfers between devices  12.7 us (6%)
  other arithmetic  11.6 us (6%)
  between operations  2.76 us (1%)
    gather x8, local copies, waits for them, and re-layouts, per_device(): recv_pos, recv_vel = ship_out(coords[:, slot_rows], velocity[:, slot_rows])  48 us
    dot_general x18, matrix products, add_block(): jnp.einsum('mh,kml->khl', high_match, spread_rows, preferred_element_type...  19.3 us
    all_to_all x2, waiting for transfers between devices, ship_back(): lax.all_to_all(buffer.reshape(3, group_size, capacity), ('wid', 'dep'), s...  12.6 us
    all_to_all x2, starting transfers between devices, ship_back(): lax.all_to_all(buffer.reshape(3, group_size, capacity), ('wid', 'dep'), s...  12 us
    all_to_all x2, starting transfers between devices, ship_out(): lax.all_to_all(positions, ('wid', 'dep'), split_axis=1, concat_axis=1, ti...  11.1 us
    gather x2, local copies, waits for them, and re-layouts, contact_buffer(): recv_pos[:, tile_facets]  10.9 us
    gather x2, local copies, waits for them, and re-layouts, contact_buffer(): recv_vel[:, tile_facets]  10.9 us
    all_to_all x2, starting transfers between devices, ship_out(): lax.all_to_all(velocities, ('wid', 'dep'), split_axis=1, concat_axis=1, t...  10.1 us
  transfers between devices with their start and end apart: 10, of which 2 were waited for; matrix products, arithmetic and copies ran while one was open for 52% of the time, Pallas kernels for 0%

commit v1 on v0

--- a/solution.py
+++ b/solution.py
@@ -13,6 +13,13 @@
 RADIUS_SQ = 1.0
 STIFFNESS = 0.1
 DAMPING = 0.05
+
+
+def exchange_blocks(block, axis, split, join):
+    peers = lax.axis_size(axis)
+    blocks = jnp.stack(jnp.split(block, peers, axis=split), axis=0)
+    blocks = lax.all_to_all(blocks, axis, split_axis=0, concat_axis=0)
+    return jnp.concatenate(blocks, axis=join)
 
 
 def from_behind(value, axis, steps):
@@ -191,7 +198,7 @@
 
 def ship_out(positions, velocities):
     recv_pos, recv_vel = (
-        lax.all_to_all(positions, ("wid", "dep"), split_axis=1, concat_axis=1, tiled=True),
+        exchange_blocks(positions, ("wid", "dep"), 1, 1),
         lax.all_to_all(velocities, ("wid", "dep"), split_axis=1, concat_axis=1, tiled=True),
     )
     return (recv_pos.reshape(3, -1), recv_vel.reshape(3, -1))

time: 199 us -> 216 us (1.085)
  local copies, waits for them, and re-layouts: 97.6 us -> 115 us
    unnamed x95 -> x125, local copies, waits for them, and re-layouts: 2.33 us -> 20.1 us
  transfers between devices with their start and end apart: 10 -> 10, of which waited for: 2 -> 2; matrix products, arithmetic and copies ran while one was open for 52% -> 42% of each run, Pallas kernels for 0% -> 0%
where the time goes in v1:
time: 216 us; the launch traced here: 215 us
  local copies, waits for them, and re-layouts  115 us (53%)
  starting transfers between devices  39.4 us (18%)
  matrix products  32.1 us (15%)
  waiting for transfers between devices  12.7 us (6%)
  other arithmetic  11.6 us (5%)
  between operations  2.77 us (1%)
    gather x8, local copies, waits for them, and re-layouts, per_device(): recv_pos, recv_vel = ship_out(coords[:, slot_rows], velocity[:, slot_rows])  46.8 us
    unnamed x125, local copies, waits for them, and re-layouts  20.1 us
    dot_general x18, matrix products, add_block(): jnp.einsum('mh,kml->khl', high_match, spread_rows, preferred_element_type...  19.3 us
    all_to_all x2, waiting for transfers between devices, ship_back(): lax.all_to_all(buffer.reshape(3, group_size, capacity), ('wid', 'dep'), s...  12.6 us
    all_to_all x2, starting transfers between devices, ship_back(): lax.all_to_all(buffer.reshape(3, group_size, capacity), ('wid', 'dep'), s...  12 us
    all_to_all x2, starting transfers between devices, exchange_blocks(): blocks = lax.all_to_all(blocks, axis, split_axis=0, concat_axis=0)  11.1 us
    gather x2, local copies, waits for them, and re-layouts, contact_buffer(): recv_pos[:, tile_facets]  10.9 us
    gather x2, local copies, waits for them, and re-layouts, contact_buffer(): recv_vel[:, tile_facets]  10.9 us
  transfers between devices with their start and end apart: 10, of which 2 were waited for; matrix products, arithmetic and copies ran while one was open for 42% of the time, Pallas kernels for 0%

profile of v1, /device:TPU:0, one launch (start us, length us, event | category | flops | bytes accessed | tf_op | source)
XLA Modules:
  0.0 214.6 jit_solution(2206209143662154894)
XLA Ops:
  0.7 1.0 copy.244
  2.4 10.8 %gather_fusion = f32[4096,3]{1,0:T(8,128)S(1)} fusion(f32[3,1024]{0,1:T(8,128)S(1)} %copy.244, s32[4096]{0:T(1024)S(1)} %broadcast_clamp_fusion), kind=kCustom, calls=%fused_computation | custom fusion | bytes 114688 | tf_op jit(solution)/shard_map/gather | solution.py:264
  23.3 7.4 %all-to-all-start = ((f32[16,3,1,256]{3,2,1,0:T(1,128)}), f32[16,3,1,256]{3,2,1,0:T(1,128)S(1)}, u32[]{:S(2)}, u32[]{:S(2)}) async-start(f32[16,3,1,256]{3,2,1,0:T(1,128)} %constant_dynamic-update-slice_fusion), calls=%async_computation | async-start | bytes 98304 | tf_op jit(solution)/shard_map/all_to_all | solution.py:21
  30.7 5.3 %collective-permute-start = (f32[3,128]{1,0:T(4,128)S(1)}, f32[3,128]{1,0:T(4,128)S(1)}, u32[]{:S(2)}, u32[]{:S(2)}) collective-permute-start(f32[3,128]{1,0:T(4,128)S(1)} %slice.69), channel_id=1, source_target_pairs={{0,31},{1,0},{2,1},{3,2},{4,3},{5,4},{6,5},{7,6},{8,7},{9,8},{10,9... | collective-permute-start | bytes 4616 | tf_op jit(solution)/shard_map/ppermute | solution.py:28
  39.4 10.8 %gather_fusion.3 = f32[4096,3]{1,0:T(8,128)S(1)} fusion(f32[3,1024]{0,1:T(8,128)S(1)} %copy.251, s32[4096]{0:T(1024)S(1)} %broadcast_clamp_fusion), kind=kCustom, calls=%fused_computation.3 | custom fusion | bytes 114688 | tf_op jit(solution)/shard_map/gather | solution.py:264
  50.2 1.2 copy.252
  51.5 1.4 fusion.100
  54.2 1.4 fusion.102
  56.2 3.5 %all-to-all-start.1 = ((f32[3,16,256]{2,0,1:T(4,128)}), f32[3,16,256]{2,0,1:T(4,128)S(1)}, u32[]{:S(2)}, u32[]{:S(2)}) async-start(f32[3,16,256]{2,0,1:T(4,128)} %bitcast.46), calls=%async_computation.1 | async-start | bytes 131072 | tf_op jit(solution)/shard_map/all_to_all | solution.py:202
  60.4 5.5 %gather_fusion.2 = f32[2048,3]{1,0:T(8,128)S(1)} fusion(f32[3,4096]{0,1:T(8,128)S(1)} %bitcast.416, s32[2048]{0:T(1024)S(1)} %broadcast_clamp_fusion.1), kind=kCustom, calls=%fused_computation.2 | custom fusion | bytes 57344 | tf_op jit(solution)/shard_map/gather | solution.py:224
  66.0 1.8 gather_fusion.1
  68.5 0.7 fusion.137
  69.9 1.6 gather_fusion.4
  71.6 5.5 %gather_fusion.5 = f32[2048,3]{1,0:T(8,128)S(1)} fusion(f32[3,4096]{0,1:T(8,128)S(1)} %bitcast.421, s32[2048]{0:T(1024)S(1)} %broadcast_clamp_fusion.1), kind=kCustom, calls=%fused_computation.5 | custom fusion | bytes 57344 | tf_op jit(solution)/shard_map/gather | solution.py:225
  77.0 1.1 copy.248
  78.1 1.8 fusion.202
  79.9 1.1 copy.255
  83.3 8.7 %while.68 = (s32[]{:T(128)}, f32[9,32,128]{2,1,0:T(8,128)S(1)}, s32[5,512]{1,0:T(8,128)}, bf16[5,9,512]{2,1,0:T(8,128)(2,1)S(1)}, s32[]{:T(128)}, /*index=5*/s32[]{:T(128)}) while((s32[]{:T(128)}, f32[9,32,128]{2,1,0:T(8,128)S(1)}, s32[5,512]{1,0:T(8,128)}, bf16[5,9,512]{2,1,0:T(8,128)(2,1)S(1)}, s32[]{:T(128)}, ...), condition=%wide.region_15.16_spmd.clone, body=%wide.region_14.15_spmd.clone.sunk | while | flops 38503936 | bytes 468063 | solution.py:140
  83.3 0.7 constant_dynamic-slice_fusion.8
  84.2 0.8 fusion.232
  85.1 0.7 constant_dynamic-slice_fusion.8
  86.0 0.8 fusion.232
  86.8 0.7 constant_dynamic-slice_fusion.8
  87.7 0.8 fusion.232
  88.6 0.7 constant_dynamic-slice_fusion.8
  89.5 0.8 fusion.232
  91.2 0.8 fusion.232
  92.8 6.0 %all-to-all-start.2 = ((f32[3,16,256]{2,0,1:T(4,128)}), f32[3,16,256]{2,0,1:T(4,128)S(1)}, u32[]{:S(2)}, u32[]{:S(2)}) async-start(f32[3,16,256]{2,0,1:T(4,128)} %bitcast.56), calls=%async_computation.2 | async-start | bytes 131072 | tf_op jit(solution)/shard_map/all_to_all | solution.py:209
  99.3 6.4 %all-to-all-done.2 = f32[3,16,256]{2,0,1:T(4,128)S(1)} async-done(((f32[3,16,256]{2,0,1:T(4,128)}), f32[3,16,256]{2,0,1:T(4,128)S(1)}, u32[]{:S(2)}, u32[]{:S(2)}) %all-to-all-start.2) | async-done | bytes 49184 | tf_op jit(solution)/shard_map/all_to_all | solution.py:209
  106.0 6.7 %while.69 = (s32[]{:T(128)}, f32[9,8,128]{2,1,0:T(8,128)S(1)}, s32[4,1024]{1,0:T(4,128)S(1)}, bf16[4,9,1024]{2,1,0:T(8,128)(2,1)S(1)}, s32[]{:T(128)}, /*index=5*/s32[]{:T(128)}) while((s32[]{:T(128)}, f32[9,8,128]{2,1,0:T(8,128)S(1)}, s32[4,1024]{1,0:T(4,128)S(1)}, bf16[4,9,1024]{2,1,0:T(8,128)(2,1)S(1)}, s32[]{:T(128)}, ...), condition=%wide.region_18.19_spmd.clone, body=%wide.region_17.18_spmd.clone.sunk | while | flops 20231172 | bytes 419935 | solution.py:140
  106.3 1.4 fusion.235
  107.9 1.4 fusion.235
  109.6 1.4 fusion.235
  111.3 1.4 fusion.235
  113.0 10.8 %gather_fusion.6 = f32[4096,3]{1,0:T(8,128)S(1)} fusion(f32[3,1024]{0,1:T(8,128)S(1)} %copy.267, s32[4096]{0:T(1024)S(1)} %broadcast_clamp_fusion), kind=kCustom, calls=%fused_computation.6 | custom fusion | bytes 114688 | tf_op jit(solution)/shard_map/gather | solution.py:264
  134.5 3.7 %all-to-all-start.3 = ((f32[16,3,1,256]{3,2,1,0:T(1,128)}), f32[16,3,1,256]{3,2,1,0:T(1,128)S(1)}, u32[]{:S(2)}, u32[]{:S(2)}) async-start(f32[16,3,1,256]{3,2,1,0:T(1,128)} %constant_dynamic-update-slice_fusion.16), calls=%async_computation.3 | async-start | bytes 98304 | tf_op jit(solution)/shard_map/all_to_all | solution.py:21
  138.1 10.8 %gather_fusion.9 = f32[4096,3]{1,0:T(8,128)S(1)} fusion(f32[3,1024]{0,1:T(8,128)S(1)} %copy.274, s32[4096]{0:T(1024)S(1)} %broadcast_clamp_fusion), kind=kCustom, calls=%fused_computation.9 | custom fusion | bytes 114688 | tf_op jit(solution)/shard_map/gather | solution.py:264
  149.0 1.2 copy.275
  150.3 1.4 fusion.101
  152.8 1.4 fusion.103
  155.0 6.7 %all-to-all-start.4 = ((f32[3,16,256]{2,0,1:T(4,128)}), f32[3,16,256]{2,0,1:T(4,128)S(1)}, u32[]{:S(2)}, u32[]{:S(2)}) async-start(f32[3,16,256]{2,0,1:T(4,128)} %bitcast.100), calls=%async_computation.4 | async-start | bytes 131072 | tf_op jit(solution)/shard_map/all_to_all | solution.py:202
  162.3 5.5 %gather_fusion.8 = f32[2048,3]{1,0:T(8,128)S(1)} fusion(f32[3,4096]{0,1:T(8,128)S(1)} %bitcast.422, s32[2048]{0:T(1024)S(1)} %broadcast_clamp_fusion.1), kind=kCustom, calls=%fused_computation.8 | custom fusion | bytes 57344 | tf_op jit(solution)/shard_map/gather | solution.py:224
  167.8 1.6 gather_fusion.7
  170.5 1.6 gather_fusion.10
  172.1 5.5 %gather_fusion.11 = f32[2048,3]{1,0:T(8,128)S(1)} fusion(f32[3,4096]{0,1:T(8,128)S(1)} %bitcast.419, s32[2048]{0:T(1024)S(1)} %broadcast_clamp_fusion.1), kind=kCustom, calls=%fused_computation.11 | custom fusion | bytes 57344 | tf_op jit(solution)/shard_map/gather | solution.py:225
  177.6 1.1 copy.271
  178.7 1.7 fusion.201
  180.4 1.1 copy.278
  183.8 8.7 %while.70 = (s32[]{:T(128)}, f32[9,32,128]{2,1,0:T(8,128)S(1)}, s32[5,512]{1,0:T(8,128)}, bf16[5,9,512]{2,1,0:T(8,128)(2,1)S(1)}, s32[]{:T(128)}, /*index=5*/s32[]{:T(128)}) while((s32[]{:T(128)}, f32[9,32,128]{2,1,0:T(8,128)S(1)}, s32[5,512]{1,0:T(8,128)}, bf16[5,9,512]{2,1,0:T(8,128)(2,1)S(1)}, s32[]{:T(128)}, ...), condition=%wide.region_35.36_spmd.clone, body=%wide.region_34.35_spmd.clone.sunk | while | flops 38503936 | bytes 468063 | solution.py:140
  184.8 0.8 fusion.238
  186.5 0.8 fusion.238
  187.3 0.7 constant_dynamic-slice_fusion.10
  188.3 0.8 fusion.238
  190.0 0.8 fusion.238
  190.8 0.7 constant_dynamic-slice_fusion.10
  191.7 0.8 fusion.238
  193.3 6.0 %all-to-all-start.5 = ((f32[3,16,256]{2,0,1:T(4,128)}), f32[3,16,256]{2,0,1:T(4,128)S(1)}, u32[]{:S(2)}, u32[]{:S(2)}) async-start(f32[3,16,256]{2,0,1:T(4,128)} %bitcast.110), calls=%async_computation.5 | async-start | bytes 131072 | tf_op jit(solution)/shard_map/all_to_all | solution.py:209
  200.0 6.3 %all-to-all-done.5 = f32[3,16,256]{2,0,1:T(4,128)S(1)} async-done(((f32[3,16,256]{2,0,1:T(4,128)}), f32[3,16,256]{2,0,1:T(4,128)S(1)}, u32[]{:S(2)}, u32[]{:S(2)}) %all-to-all-start.5) | async-done | bytes 49184 | tf_op jit(solution)/shard_map/all_to_all | solution.py:209
  206.5 6.7 %while.71 = (s32[]{:T(128)}, f32[9,8,128]{2,1,0:T(8,128)S(1)}, s32[4,1024]{1,0:T(4,128)S(1)}, bf16[4,9,1024]{2,1,0:T(8,128)(2,1)S(1)}, s32[]{:T(128)}, /*index=5*/s32[]{:T(128)}) while((s32[]{:T(128)}, f32[9,8,128]{2,1,0:T(8,128)S(1)}, s32[4,1024]{1,0:T(4,128)S(1)}, bf16[4,9,1024]{2,1,0:T(8,128)(2,1)S(1)}, s32[]{:T(128)}, ...), condition=%wide.region_38.39_spmd.clone, body=%wide.region_37.38_spmd.clone.sunk | while | flops 20231172 | bytes 419935 | solution.py:140
  206.8 1.4 fusion.241
  208.5 1.4 fusion.241
  210.1 1.4 fusion.241
  211.8 1.4 fusion.241
  213.3 1.3 multiply_add_fusion
  (339 shorter events, 45.6 us)
Async XLA Ops:
  0.6 37.8 %copy-start.14 = (s32[1,16,256]{2,1,0:T(8,128)S(1)}, s32[1,16,256]{2,1,0:T(8,128)}, u32[]{:S(2)}) copy-start(s32[1,16,256]{2,1,0:T(8,128)} %param.31) | copy-start | bytes 49156
  0.6 30.1 %copy-start.1 = (f32[3,1024]{1,0:T(4,128)S(1)}, f32[3,1024]{1,0:T(4,128)}, u32[]{:S(2)}) copy-start(f32[3,1024]{1,0:T(4,128)} %param.24) | copy-start | bytes 36868
  0.7 35.4 %copy-start.28 = (s32[4,4,128]{2,1,0:T(4,128)S(1)}, s32[4,4,128]{2,1,0:T(4,128)}, u32[]{:S(2)}) copy-start(s32[4,4,128]{2,1,0:T(4,128)} %param.34) | copy-start | bytes 24580
  0.7 35.4 %copy-start.38 = (s32[4,128]{1,0:T(4,128)S(1)}, s32[4,128]{1,0:T(4,128)}, u32[]{:S(2)}) copy-start(s32[4,128]{1,0:T(4,128)} %param.33) | copy-start | bytes 6148
  0.7 36.7 %copy-start.37 = (f32[2,1024]{1,0:T(2,128)S(1)}, f32[2,1024]{1,0:T(2,128)}, u32[]{:S(2)}) copy-start(f32[2,1024]{1,0:T(2,128)} %param.28) | copy-start | bytes 24580
  0.7 36.9 %copy-start.39 = (f32[1024]{0:T(1024)S(1)}, f32[1024]{0:T(1024)}, u32[]{:S(2)}) copy-start(f32[1024]{0:T(1024)} %param.29) | copy-start | bytes 12292
  0.7 37.0 %copy-start.33 = (s32[4,1024]{1,0:T(4,128)S(1)}, s32[4,1024]{1,0:T(4,128)}, u32[]{:S(2)}) copy-start(s32[4,1024]{1,0:T(4,128)} %param.26) | copy-start | bytes 49156
  23.3 32.9 %all-to-all-start = ((f32[16,3,1,256]{3,2,1,0:T(1,128)}), f32[16,3,1,256]{3,2,1,0:T(1,128)S(1)}, u32[]{:S(2)}, u32[]{:S(2)}) async-start(f32[16,3,1,256]{3,2,1,0:T(1,128)} %constant_dynamic-update-slice_fusion), calls=%async_computation | async-start | bytes 98304 | tf_op jit(solution)/shard_map/all_to_all | solution.py:21
  30.7 20.7 %collective-permute-start = (f32[3,128]{1,0:T(4,128)S(1)}, f32[3,128]{1,0:T(4,128)S(1)}, u32[]{:S(2)}, u32[]{:S(2)}) collective-permute-start(f32[3,128]{1,0:T(4,128)S(1)} %slice.69), channel_id=1, source_target_pairs={{0,31},{1,0},{2,1},{3,2},{4,3},{5,4},{6,5},{7,6},{8,7},{9,8},{10,9... | collective-permute-start | bytes 4616 | tf_op jit(solution)/shard_map/ppermute | solution.py:28
  37.8 16.0 %copy-start.3 = (f32[3,1024]{1,0:T(4,128)}, f32[3,1024]{1,0:T(4,128)S(1)}, u32[]{:S(2)}) copy-start(f32[3,1024]{1,0:T(4,128)S(1)} %pad_maximum_fusion.10) | copy-start | bytes 36868
  37.9 16.0 %copy-start.7 = (f32[3,1024]{1,0:T(4,128)}, f32[3,1024]{1,0:T(4,128)S(1)}, u32[]{:S(2)}) copy-start(f32[3,1024]{1,0:T(4,128)S(1)} %maximum_maximum_fusion) | copy-start | bytes 36868
  50.1 3.0 %copy-start = (f32[8,1024]{1,0:T(8,128)S(1)}, f32[8,1024]{1,0:T(8,128)}, u32[]{:S(2)}) copy-start(f32[8,1024]{1,0:T(8,128)} %param.27) | copy-start | bytes 98308
  50.1 3.1 %copy-start.36 = (f32[3,1024]{1,0:T(4,128)S(1)}, f32[3,1024]{1,0:T(4,128)}, u32[]{:S(2)}) copy-start(f32[3,1024]{1,0:T(4,128)} %param.30) | copy-start | bytes 36868
  50.2 3.1 %copy-start.41 = (f32[4]{0:T(128)S(1)}, f32[4]{0:T(128)}, u32[]{:S(2)}) copy-start(f32[4]{0:T(128)} %constant.306.clone) | copy-start | bytes 52
  51.4 4.2 %copy-start.34 = (s32[4,8,128]{2,0,1:T(4,128)}, s32[4,8,128]{2,0,1:T(4,128)S(1)}, u32[]{:S(2)}) copy-start(s32[4,8,128]{2,0,1:T(4,128)S(1)} %copy.240) | copy-start | bytes 49156
  53.3 0.6 copy-start.19
  53.3 0.6 copy-start.21
  53.4 0.6 copy-start.29
  56.2 13.0 %all-to-all-start.1 = ((f32[3,16,256]{2,0,1:T(4,128)}), f32[3,16,256]{2,0,1:T(4,128)S(1)}, u32[]{:S(2)}, u32[]{:S(2)}) async-start(f32[3,16,256]{2,0,1:T(4,128)} %bitcast.46), calls=%async_computation.1 | async-start | bytes 131072 | tf_op jit(solution)/shard_map/all_to_all | solution.py:202
  66.0 4.0 %copy-start.17 = (s32[1024]{0:T(1024)S(1)}, s32[1024]{0:T(1024)}, u32[]{:S(2)}) copy-start(s32[1024]{0:T(1024)} %pad_clamp_fusion) | copy-start | bytes 12292
  69.9 11.3 %copy-start.27 = (f32[4,128,3]{1,2,0:T(4,128)S(1)}, f32[4,128,3]{1,2,0:T(4,128)}, u32[]{:S(2)}) copy-start(f32[4,128,3]{1,2,0:T(4,128)} %copy.257) | copy-start | bytes 18436
  80.9 2.3 %copy-start.10 = (f32[9,32,128]{2,1,0:T(8,128)S(1)}, f32[9,32,128]{2,1,0:T(8,128)}, u32[]{:S(2)}) copy-start(f32[9,32,128]{2,1,0:T(8,128)} %custom-call) | copy-start | bytes 442372
  83.3 15.5 %copy-start.15 = (f32[3,8,128]{2,1,0:T(8,128)S(1)}, f32[3,8,128]{2,1,0:T(8,128)}, u32[]{:S(2)}) copy-start(f32[3,8,128]{2,1,0:T(8,128)} %get-tuple-element.619) | copy-start | bytes 36868
  83.3 15.5 %copy-start.16 = (f32[3,8,128]{2,1,0:T(8,128)S(1)}, f32[3,8,128]{2,1,0:T(8,128)}, u32[]{:S(2)}) copy-start(f32[3,8,128]{2,1,0:T(8,128)} %get-tuple-element.620) | copy-start | bytes 36868
  83.3 22.6 %copy-start.26 = (f32[9,8,128]{2,1,0:T(8,128)S(1)}, f32[9,8,128]{2,1,0:T(8,128)}, u32[]{:S(2)}) copy-start(f32[9,8,128]{2,1,0:T(8,128)} %custom-call.1) | copy-start | bytes 110596
  92.8 12.9 %all-to-all-start.2 = ((f32[3,16,256]{2,0,1:T(4,128)}), f32[3,16,256]{2,0,1:T(4,128)S(1)}, u32[]{:S(2)}, u32[]{:S(2)}) async-start(f32[3,16,256]{2,0,1:T(4,128)} %bitcast.56), calls=%async_computation.2 | async-start | bytes 131072 | tf_op jit(solution)/shard_map/all_to_all | solution.py:209
  98.8 13.9 %collective-permute-start.1 = (f32[3,128]{1,0:T(4,128)S(1)}, f32[3,128]{1,0:T(4,128)S(1)}, u32[]{:S(2)}, u32[]{:S(2)}) collective-permute-start(f32[3,128]{1,0:T(4,128)S(1)} %slice.115), channel_id=1, source_target_pairs={{0,1},{1,2},{2,3},{3,4},{4,5},{5,6},{6,7},{7,8},{8,9},{9,10},{10,1... | collective-permute-start | bytes 4616 | tf_op jit(solution)/shard_map/ppermute | solution.py:28
  105.9 6.8 %copy-start.2 = (f32[3,1024]{1,0:T(4,128)S(1)}, f32[3,1024]{1,0:T(4,128)}, u32[]{:S(2)}) copy-start(f32[3,1024]{1,0:T(4,128)} %param.24) | copy-start | bytes 36868
  106.0 6.8 %copy-start.13 = (f32[3,1024]{1,0:T(4,128)S(1)}, f32[3,1024]{1,0:T(4,128)}, u32[]{:S(2)}) copy-start(f32[3,1024]{1,0:T(4,128)} %param.23) | copy-start | bytes 36868
  106.0 6.8 %copy-start.31 = (f32[1024]{0:T(1024)S(1)}, f32[1024]{0:T(1024)}, u32[]{:S(2)}) copy-start(f32[1024]{0:T(1024)} %param.25) | copy-start | bytes 12292
  112.8 11.0 %copy-start.5 = (f32[3,1024]{1,0:T(4,128)}, f32[3,1024]{1,0:T(4,128)S(1)}, u32[]{:S(2)}) copy-start(f32[3,1024]{1,0:T(4,128)S(1)} %get-tuple-element.603) | copy-start | bytes 36868
  124.4 25.9 %copy-start.35 = (s32[4,8,128]{2,0,1:T(4,128)S(1)}, s32[4,8,128]{2,0,1:T(4,128)}, u32[]{:S(2)}) copy-start(s32[4,8,128]{2,0,1:T(4,128)} %copy-done.34) | copy-start | bytes 49156
  133.3 16.9 %collective-permute-start.2 = (f32[3,128]{1,0:T(4,128)S(1)}, f32[3,128]{1,0:T(4,128)S(1)}, u32[]{:S(2)}, u32[]{:S(2)}) collective-permute-start(f32[3,128]{1,0:T(4,128)S(1)} %slice.116), channel_id=1, source_target_pairs={{0,31},{1,0},{2,1},{3,2},{4,3},{5,4},{6,5},{7,6},{8,7},{9,8},{10,9... | collective-permute-start | bytes 4616 | tf_op jit(solution)/shard_map/ppermute | solution.py:28
  134.5 20.5 %all-to-all-start.3 = ((f32[16,3,1,256]{3,2,1,0:T(1,128)}), f32[16,3,1,256]{3,2,1,0:T(1,128)S(1)}, u32[]{:S(2)}, u32[]{:S(2)}) async-start(f32[16,3,1,256]{3,2,1,0:T(1,128)} %constant_dynamic-update-slice_fusion.16), calls=%async_computation.3 | async-start | bytes 98304 | tf_op jit(solution)/shard_map/all_to_all | solution.py:21
  148.9 3.0 %copy-start.4 = (f32[3,1024]{1,0:T(4,128)S(1)}, f32[3,1024]{1,0:T(4,128)}, u32[]{:S(2)}) copy-start(f32[3,1024]{1,0:T(4,128)} %copy-done.3) | copy-start | bytes 36868
  148.9 3.0 %copy-start.8 = (f32[3,1024]{1,0:T(4,128)S(1)}, f32[3,1024]{1,0:T(4,128)}, u32[]{:S(2)}) copy-start(f32[3,1024]{1,0:T(4,128)} %copy-done.7) | copy-start | bytes 36868
  148.9 3.1 %copy-start.20 = (f32[1,1024]{1,0:T(1,128)S(1)}, f32[1,1024]{1,0:T(1,128)}, u32[]{:S(2)}) copy-start(f32[1,1024]{1,0:T(1,128)} %copy-done.19) | copy-start | bytes 12292
  149.0 3.1 %copy-start.22 = (f32[1,1024]{1,0:T(1,128)S(1)}, f32[1,1024]{1,0:T(1,128)}, u32[]{:S(2)}) copy-start(f32[1,1024]{1,0:T(1,128)} %copy-done.21) | copy-start | bytes 12292
  149.0 3.2 %copy-start.30 = (f32[4,1024]{1,0:T(4,128)S(1)}, f32[4,1024]{1,0:T(4,128)}, u32[]{:S(2)}) copy-start(f32[4,1024]{1,0:T(4,128)} %copy-done.29) | copy-start | bytes 49156
  149.0 3.2 %copy-start.42 = (f32[4]{0:T(128)S(1)}, f32[4]{0:T(128)}, u32[]{:S(2)}) copy-start(f32[4]{0:T(128)} %constant.306.clone) | copy-start | bytes 52
  152.1 0.6 copy-start.23
  152.7 15.0 %copy-start.18 = (s32[1024]{0:T(1024)S(1)}, s32[1024]{0:T(1024)}, u32[]{:S(2)}) copy-start(s32[1024]{0:T(1024)} %pad_clamp_fusion) | copy-start | bytes 12292
  154.3 15.5 %copy-start.11 = (f32[1,3,9,128]{3,1,2,0:T(4,128)}, f32[1,3,9,128]{3,1,2,0:T(4,128)S(1)}, u32[]{:S(2)}) copy-start(f32[1,3,9,128]{3,1,2,0:T(4,128)S(1)} %copy.314) | copy-start | bytes 41476
  154.9 58.4 %collective-permute-start.3 = (f32[3,128]{1,0:T(4,128)}, f32[3,128]{1,0:T(4,128)}, u32[]{:S(2)}, u32[]{:S(2)}) collective-permute-start(f32[3,128]{1,0:T(4,128)} %slice.122), channel_id=1, source_target_pairs={{0,1},{1,2},{2,3},{3,4},{4,5},{5,6},{6,7},{7,8},{8,9},{9,10},{10,1... | collective-permute-start | bytes 4616 | tf_op jit(solution)/shard_map/ppermute | solution.py:28
  155.0 14.8 %all-to-all-start.4 = ((f32[3,16,256]{2,0,1:T(4,128)}), f32[3,16,256]{2,0,1:T(4,128)S(1)}, u32[]{:S(2)}, u32[]{:S(2)}) async-start(f32[3,16,256]{2,0,1:T(4,128)} %bitcast.100), calls=%async_computation.4 | async-start | bytes 131072 | tf_op jit(solution)/shard_map/all_to_all | solution.py:202
  169.4 9.2 %copy-start.40 = (f32[4]{0:T(128)S(1)}, f32[4]{0:T(128)}, u32[]{:S(2)}) copy-start(f32[4]{0:T(128)} %compare_convert_fusion) | copy-start | bytes 52
  181.5 2.3 %copy-start.9 = (f32[9,32,128]{2,1,0:T(8,128)S(1)}, f32[9,32,128]{2,1,0:T(8,128)}, u32[]{:S(2)}) copy-start(f32[9,32,128]{2,1,0:T(8,128)} %custom-call.2) | copy-start | bytes 442372
  183.8 15.5 %copy-start.24 = (f32[1,1024]{1,0:T(1,128)S(1)}, f32[1,1024]{1,0:T(1,128)}, u32[]{:S(2)}) copy-start(f32[1,1024]{1,0:T(1,128)} %copy-done.23) | copy-start | bytes 12292
  183.8 22.7 %copy-start.25 = (f32[9,8,128]{2,1,0:T(8,128)S(1)}, f32[9,8,128]{2,1,0:T(8,128)}, u32[]{:S(2)}) copy-start(f32[9,8,128]{2,1,0:T(8,128)} %custom-call.3) | copy-start | bytes 110596
  193.3 12.9 %all-to-all-start.5 = ((f32[3,16,256]{2,0,1:T(4,128)}), f32[3,16,256]{2,0,1:T(4,128)S(1)}, u32[]{:S(2)}, u32[]{:S(2)}) async-start(f32[3,16,256]{2,0,1:T(4,128)} %bitcast.110), calls=%async_computation.5 | async-start | bytes 131072 | tf_op jit(solution)/shard_map/all_to_all | solution.py:209
  206.5 6.8 %copy-start.6 = (f32[3,1024]{1,0:T(4,128)S(1)}, f32[3,1024]{1,0:T(4,128)}, u32[]{:S(2)}) copy-start(f32[3,1024]{1,0:T(4,128)} %copy-done.5) | copy-start | bytes 36868
  206.5 6.8 %copy-start.12 = (f32[1,3,9,128]{3,1,2,0:T(4,128)S(1)}, f32[1,3,9,128]{3,1,2,0:T(4,128)}, u32[]{:S(2)}) copy-start(f32[1,3,9,128]{3,1,2,0:T(4,128)} %copy-done.11) | copy-start | bytes 41476
  206.5 6.8 %copy-start.32 = (f32[1024]{0:T(1024)S(1)}, f32[1024]{0:T(1024)}, u32[]{:S(2)}) copy-start(f32[1024]{0:T(1024)} %param.25) | copy-start | bytes 12292
